TPU v7x, 32 devices: a 4x4x1 block of a 4x4x8 slice. The times are simulated.
32 devices in a mesh: dp: 1 (over z), ep: 32 (over y, x, core).
Axes of the slice: x: 4, y: 4, z: 1, core: 2. Of those that a mesh axis runs over, the one named last changes fastest.
The devices are a block of a 4x4x8 slice.
Arguments:
- hidden: bfloat16 [32768, 1024], P(('dp', 'ep'))
- route_idx: int32 [32768, 8], P(('dp', 'ep'))
- gate_weights: float32 [32768, 8], P(('dp', 'ep'))
- w_gate: bfloat16 [32, 1024, 512], P('ep')
- w_up: bfloat16 [32, 1024, 512], P('ep')
- w_down: bfloat16 [32, 512, 1024], P('ep')
Outputs:
- output: bfloat16 [32768, 1024], P(('dp', 'ep'))
All inputs are finite; a program needn't handle non-finite values.
Results may differ from a plain program's by a relative error of at most 0.001.
Values are sent between devices in bfloat16 or wider.
A program may use at most 768 MiB of HBM per device.

v0:
```python
import jax
import jax.numpy as jnp
from jax import lax
from jax.sharding import PartitionSpec as P, NamedSharding


def pair_plan(route_rows, num_experts, row_cap):
    tok_count, top_k = route_rows.shape
    flat_ids = route_rows.reshape(-1)
    sort_order = jnp.argsort(flat_ids, stable=True)
    counts = jnp.bincount(flat_ids, length=num_experts)
    starts = jnp.cumsum(counts) - counts
    slot_range = jnp.arange(row_cap)
    pair_pos = jnp.minimum(starts[:, None] + slot_range[None, :], tok_count * top_k - 1)
    src_rows = sort_order[pair_pos] // top_k
    pair_rank = jnp.argsort(sort_order) - starts[flat_ids]
    return src_rows, flat_ids, pair_rank


def expert_ffn(rows_in, w_gate, w_up, w_down):
    gate_proj = jnp.einsum('lscd,ldf->lscf', rows_in, w_gate, preferred_element_type=jnp.float32)
    up_proj = jnp.einsum('lscd,ldf->lscf', rows_in, w_up, preferred_element_type=jnp.float32)
    hidden_act = (jax.nn.silu(gate_proj) * up_proj).astype(jnp.bfloat16)
    return jnp.einsum('lscf,lfd->lscd', hidden_act, w_down, preferred_element_type=jnp.float32).astype(jnp.bfloat16)


def solution(mesh):
    ep_size = mesh.shape['ep']

    def device_body(hidden, route_idx, gate_weights, w_gate, w_up, w_down):
        tok_count, top_k = route_idx.shape
        d_model = hidden.shape[1]
        local_experts = w_gate.shape[0]
        num_experts = local_experts * ep_size
        row_cap = min(tok_count, 4 * top_k * tok_count // num_experts)
        src_rows, flat_ids, pair_rank = pair_plan(route_idx, num_experts, row_cap)
        send_idx = src_rows.reshape(ep_size, local_experts, row_cap).transpose(1, 0, 2)
        send_rows = hidden[send_idx]
        recv_rows = lax.all_to_all(send_rows, 'ep', 1, 1, tiled=True)
        expert_out = expert_ffn(recv_rows, w_gate, w_up, w_down)
        back_rows = lax.all_to_all(expert_out, 'ep', 1, 1, tiled=True)
        slot_pos = (flat_ids % local_experts) * (ep_size * row_cap) + (flat_ids // local_experts) * row_cap + pair_rank
        picked = back_rows.reshape(-1, d_model)[slot_pos].reshape(tok_count, top_k, d_model)
        mixed_out = jnp.sum(gate_weights[:, :, None] * picked, axis=1)
        return mixed_out.astype(jnp.bfloat16)

    row_spec = P(('dp', 'ep'), None)
    expert_spec = P('ep', None, None)
    return jax.shard_map(device_body, mesh=mesh, in_specs=(row_spec, row_spec, row_spec, expert_spec, expert_spec, expert_spec), out_specs=row_spec, check_vma=False)
```

profile of v0, /device:TPU:107, one launch (start us, length us, event | category | flops | bytes accessed | tf_op | source)
XLA Modules:
  0.0 2434.9 jit_solution(15590169262095216036)
XLA Ops:
  0.0 1.1 copy.14
  1.1 0.3 reshape.208
  1.4 0.3 reshape.207
  1.7 57.0 %scatter_custom_fusion = s32[32]{0:T(128)S(1)} fusion(s32[8192]{0:T(1024)S(1)} %bitcast.85, s32[8192]{0:T(1024)S(1)} %broadcast.242, s32[]{:T(128)} %constant.52.clone.1), kind=kCustom, calls=%fused_computation.66 | custom fusion | flops 8192 | bytes 132 | tf_op jit(solution)/shard_map/scatter-add | solution.py:11
  58.9 0.1 reduce
  59.0 0.1 fusion.15
  59.2 0.4 copy-done.3
  59.5 6.8 sort.34
  66.3 180.5 %gather_fusion = s32[32768]{0:T(1024)S(1)} fusion(s32[8192]{0:T(1024)S(1)} %get-tuple-element.7, s32[32768]{0:T(1024)S(1)} %broadcast_clamp_fusion.1), kind=kCustom, calls=%fused_computation | custom fusion | bytes 393216 | tf_op jit(solution)/shard_map/gather | solution.py:15
  247.1 138.5 %gather_fusion.1 = bf16[32768,1024]{1,0:T(8,128)(2,1)} fusion(bf16[1024,1024]{1,0:T(8,128)(2,1)S(1)} %copy-done, s32[32768]{0:T(1024)S(1)} %broadcast_clamp_fusion), kind=kCustom, calls=%fused_computation.1 | custom fusion | bytes 134348800 | tf_op jit(solution)/shard_map/gather | solution.py:38
  385.5 816.6 %all_to_all.10 = bf16[1,32,1024,1024]{3,2,0,1:T(8,128)(2,1)} all-to-all(bf16[1,32,1024,1024]{3,2,0,1:T(8,128)(2,1)} %bitcast.3), channel_id=1, replica_groups=mesh['dp'=1,'ep'=32] {'ep'}, dimensions={1} | all-to-all | bytes 134217728 | tf_op jit(solution)/shard_map/all_to_all | solution.py:39
  1202.2 57.3 %fusion.2 = f32[32,1024,512]{2,1,0:T(8,128)} fusion(bf16[1,32,1024,1024]{3,2,0,1:T(8,128)(2,1)} %all_to_all.10, bf16[1,1024,512]{2,1,0:T(8,128)(2,1)S(1)} %copy-done.10), kind=kOutput, calls=%fused_computation.6 | convolution fusion | flops 34359738368 | bytes 135266304 | tf_op jit(solution)/shard_map/lscd,ldf->lscf/dot_general | solution.py:21
  1259.5 88.1 %convert_bitcast_fusion = bf16[1,32,1024,1024]{3,2,0,1:T(8,128)(2,1)} fusion(f32[32,1024,512]{2,1,0:T(8,128)} %fusion.2, bf16[1,32,1024,1024]{3,2,0,1:T(8,128)(2,1)} %all_to_all.10, bf16[1,512,1024]{2,1,0:T(8,128)(2,1)} %param.11, bf16[1,1024,512]{2,1,0:T(8,128)(2,1)} %param.10), kind=kOutput, calls=%fused_computation.8 | convolution fusion | flops 68853694464 | bytes 203423744 | tf_op jit(solution)/shard_map/lscf,lfd->lscd/dot_general | solution.py:24
  1347.6 23.8 all-to-all-start.1
  1371.4 6.8 sort.35
  1378.2 0.2 copy.13
  1378.4 0.7 fusion.24
  1379.1 0.7 fusion.23
  1379.9 4.5 compare_select_fusion.3
  1384.4 2.5 compare_reduce_fusion.24
  1386.9 15.7 fusion.18
  1402.6 867.1 %all-to-all-done.1 = bf16[1,32,1024,1024]{3,2,0,1:T(8,128)(2,1)} async-done(((bf16[1,32,1024,1024]{3,2,0,1:T(8,128)(2,1)}), bf16[1,32,1024,1024]{3,2,0,1:T(8,128)(2,1)}, u32[]{:S(2)}, u32[]{:S(2)}) %all-to-all-start.1) | async-done | bytes 67108896 | tf_op jit(solution)/shard_map/all_to_all | solution.py:41
  2269.6 150.5 %gather_fusion.2 = bf16[8192,1024]{1,0:T(8,128)(2,1)} fusion(bf16[32768,1024]{1,0:T(8,128)(2,1)} %bitcast.13, s32[8192]{0:T(1024)S(1)} %fusion.18), kind=kCustom, calls=%fused_computation.2 | custom fusion | bytes 33587200 | tf_op jit(solution)/shard_map/gather | solution.py:43
  2420.1 14.8 fusion.4
  (34 shorter events, 0.5 us)
Async XLA Ops:
  0.0 247.1 %copy-start = (bf16[1024,1024]{1,0:T(8,128)(2,1)S(1)}, bf16[1024,1024]{1,0:T(8,128)(2,1)}, u32[]{:S(2)}) copy-start(bf16[1024,1024]{1,0:T(8,128)(2,1)} %param.6) | copy-start | bytes 6291460
  1.4 245.4 %copy-start.5 = (s32[8192,1]{0,1:T(1,128)}, s32[8192,1]{0,1:T(1,128)S(1)}, u32[]{:S(2)}) copy-start(s32[8192,1]{0,1:T(1,128)S(1)} %reshape.208) | copy-start | bytes 98308
  1.7 245.2 %copy-start.7 = (s32[8192]{0:T(1024)}, s32[8192]{0:T(1024)S(1)}, u32[]{:S(2)}) copy-start(s32[8192]{0:T(1024)S(1)} %reshape.207) | copy-start | bytes 98308
  59.0 0.5 copy-start.3
  66.3 180.6 %copy-start.1 = (s32[8192]{0:T(1024)}, s32[8192]{0:T(1024)S(1)}, u32[]{:S(2)}) copy-start(s32[8192]{0:T(1024)S(1)} %get-tuple-element.7) | copy-start | bytes 98308
  385.5 816.6 %copy-start.10 = (bf16[1,1024,512]{2,1,0:T(8,128)(2,1)S(1)}, bf16[1,1024,512]{2,1,0:T(8,128)(2,1)}, u32[]{:S(2)}) copy-start(bf16[1,1024,512]{2,1,0:T(8,128)(2,1)} %param.9) | copy-start | bytes 3145732
  1347.6 23.9 copy-start.2
  1347.6 30.6 %copy-start.9 = (f32[1024,8]{0,1:T(8,128)S(1)}, f32[1024,8]{0,1:T(8,128)}, u32[]{:S(2)}) copy-start(f32[1024,8]{0,1:T(8,128)} %param.8) | copy-start | bytes 98308
  1347.6 30.8 %copy-start.4 = (s32[32]{0:T(128)S(1)}, s32[32]{0:T(128)}, u32[]{:S(2)}) copy-start(s32[32]{0:T(128)} %copy-done.3) | copy-start | bytes 388
  1347.6 32.3 %copy-start.6 = (s32[8192,1]{0,1:T(1,128)S(1)}, s32[8192,1]{0,1:T(1,128)}, u32[]{:S(2)}) copy-start(s32[8192,1]{0,1:T(1,128)} %copy-done.5) | copy-start | bytes 98308
  1347.6 39.3 %copy-start.8 = (s32[8192]{0:T(1024)S(1)}, s32[8192]{0:T(1024)}, u32[]{:S(2)}) copy-start(s32[8192]{0:T(1024)} %copy-done.7) | copy-start | bytes 98308
  1347.6 922.0 %all-to-all-start.1 = ((bf16[1,32,1024,1024]{3,2,0,1:T(8,128)(2,1)}), bf16[1,32,1024,1024]{3,2,0,1:T(8,128)(2,1)}, u32[]{:S(2)}, u32[]{:S(2)}) async-start(bf16[1,32,1024,1024]{3,2,0,1:T(8,128)(2,1)} %convert_bitcast_fusion), calls=%async_computation.1 | async-start | bytes 134217728 | tf_op jit(solution)/shard_map/all_to_all | solution.py:41
where the time goes:
time: 2440 us; the launch traced here: 2430 us
  waiting for transfers between devices  867 us (36%)
  blocking collectives  817 us (33%)
  local copies, waits for them, and re-layouts  473 us (19%)
  matrix products  145 us (6%)
  other arithmetic  108 us (4%)
    all_to_all x1, waiting for transfers between devices, device_body(): back_rows = lax.all_to_all(expert_out, 'ep', 1, 1, tiled=True)  867 us
    all_to_all x1, blocking collectives, device_body(): recv_rows = lax.all_to_all(send_rows, 'ep', 1, 1, tiled=True)  817 us
    gather x2, local copies, waits for them, and re-layouts, pair_plan(): src_rows = sort_order[pair_pos] // top_k  181 us
    gather x1, local copies, waits for them, and re-layouts, device_body(): back_rows.reshape(-1, d_model)[slot_pos].reshape(tok_count, top_k, d_model)  150 us
    gather x1, local copies, waits for them, and re-layouts, device_body(): send_rows = hidden[send_idx]  138 us
    dot_general x1, matrix products, expert_ffn(): jnp.einsum('lscf,lfd->lscd', hidden_act, w_down, preferred_element_type=j...  88.1 us
    dot_general x1, matrix products, expert_ffn(): jnp.einsum('lscd,ldf->lscf', rows_in, w_gate, preferred_element_type=jnp....  57.3 us
    scatter-add x1, other arithmetic, pair_plan(): counts = jnp.bincount(flat_ids, length=num_experts)  57 us
  transfers between devices with their start and end apart: 1, of which 1 were waited for; matrix products, arithmetic and copies ran while one was open for 1% of the time, Pallas kernels for 0%

commit v1 on v0

v1 whole, which is shorter than its diff:
```python
import heapq
import math

import jax
import jax.numpy as jnp
from jax import lax
from jax.experimental import pallas as pl
from jax.experimental.pallas import tpu as pltpu
from jax.sharding import PartitionSpec as P

MESH = pl.DeviceIdType.MESH
BF16, F32 = jnp.bfloat16, jnp.float32
BOTH = (0, 1)
SIDES = (-1, 1)
DIRS = (1, -1)
GROUP = 4
LANES = 128
BLOCK = 2 * LANES
HELD = 16
PIECES = 32
ROWS = (0, 1, -1, 2)
CHUNKS = ((0, 256), (256, 256), (512, 256), (768, 128), (896, 128))
DETOUR = ()
LEAD = 12
SEGMENTS = (('o', LEAD), ('opp', LEAD - 2), ('op', 34 - 2 * LEAD), ('p', 2))
ORDER = ('W0', 'W1', 'G0', 'D0', 'T0', 'D1', 'd0', 'T1', 'R0', 'R1', 'd1', 'd2', 'd3', 'd4', 'P0', 'P1', 'P2', 'P3', 'P4',
         'F0', 'S0', 'F1', 'S1', 'f0', 's0', 'f1', 's1', 'f2', 's2', 'f3', 's3', 'f4', 's4')
RANK = {name: i for i, name in enumerate(ORDER)}
RATE, LATENCY, CHIP_RATE, CHIP_LATENCY = 45.6e3, 2.3, 400e3, 1.8
STEP_US, UNIT_US, FINAL_US, START_US, AHEAD_US = 1.28, 1.65, 0.6, 5.0, 4.0
NEVER, TICK_US = 1e9, 0.01


def make_steps():
    steps, base = [], {'o': 0, 'p': 0}
    for pattern, count in SEGMENTS:
        for ch in pattern * count:
            steps.append((ch, base[ch]))
            base[ch] += 1
    return steps


STEPS = make_steps()


class Planner:
    def __init__(self, piece_bytes, down_bytes, token_bytes, gate_bytes, sum_bytes):
        self.t, self.free, self.arr, self.ready, self.done, self.out = START_US, {}, {}, {}, set(), []
        self.piece, self.sum = piece_bytes, sum_bytes
        self.down = [down_bytes * w for _, w in CHUNKS]
        for n in SIDES:
            self.push(('x', n), gate_bytes, ('G', 0, n))
            for q in BOTH:
                self.push(('x', n), token_bytes, ('T', q, n))
            for k in BOTH:
                for d in DIRS:
                    for h in BOTH:
                        self.push(('x', n), piece_bytes, ('D', k, d, -n, h))
            for i, size in enumerate(self.down):
                for h in BOTH:
                    self.push(('x', n), size, ('d', i, -n, h))
        for h, d in zip(BOTH, DIRS):
            for k in BOTH:
                for part in BOTH:
                    self.push(('y', d), piece_bytes, ('W', k, d, part))
            for i in DETOUR:
                self.push(('y', d), self.down[i], ('w', i, h))

    def push(self, link, size, key):
        name, i, *_ = key
        queue = self.ready.setdefault(link, [])
        heapq.heappush(queue, (RANK.get(name + str(i), 0), len(self.arr) + len(queue) + len(self.out), size, key))

    def fill(self):
        for link, queue in self.ready.items():
            chip = link == 'chip'
            while queue and (chip or self.free.get(link, START_US) - self.t < AHEAD_US):
                _, _, size, key = heapq.heappop(queue)
                self.free[link] = max(self.t, self.free.get(link, START_US)) + size / (CHIP_RATE if chip else RATE)
                self.arr[key] = self.free[link] + (CHIP_LATENCY if chip else LATENCY)
                self.out.append(('send', key))

    def event(self, key):
        self.t = max(self.t, self.arr[key])
        self.out.append(('wait', key))
        self.done.add(key)
        t, i, *rest = key
        if t == 'W':
            d, h = rest
            for n in SIDES:
                self.push(('x', n), self.piece, ('R', i, d, -n, h))
        elif t in ('D', 'R', 'S', 'F'):
            d, n, h = rest
            if t == 'D':
                self.push(('y', -d), self.piece, ('S', i, d, n, h))
            if t == 'R':
                self.push(('y', d), self.piece, ('F', i, d, n, h))
            if (t, i, d, n, not h) in self.done:
                self.push('chip', 2 * self.piece, ('B', t, i, d, n))
        elif t == 'w':
            h, = rest
            for n in SIDES:
                self.push(('x', n), self.down[i], ('r', i, -n, h))
        elif t in ('d', 'r', 's', 'f'):
            n, *dy, h = rest
            d = DIRS[h]
            if t == 'd':
                for to in (-d,) if i in DETOUR else DIRS:
                    self.push(('y', to), self.down[i], ('s', i, n, -to, h))
                dy = 0
            elif t == 'f':
                dy = 2
            else:
                dy = dy[0] if dy else -d
                if dy == -d:
                    self.push(('y', d), self.down[i], ('f', i, n, h))
            self.done.add((i, n, dy, h))
            if (i, n, dy, not h) in self.done:
                self.push('chip', 2 * self.down[i], ('b', i, n, dy))
        self.fill()

    def next_event(self):
        waiting = [(a, k) for k, a in self.arr.items() if k not in self.done and k[0] not in 'BbTGP']
        return min(waiting, key=lambda z: z[0], default=None)

    def poll(self):
        self.fill()
        while (p := self.next_event()) and p[0] <= self.t:
            self.event(p[1])
        self.fill()

    def advance(self, upto=NEVER):
        p = self.next_event()
        c = [self.free.get(link, START_US) - AHEAD_US + TICK_US for link, queue in self.ready.items() if queue]
        self.t = max(self.t, min([p[0] if p else NEVER, upto] + c))
        self.poll()

    def need(self, key):
        while key not in self.done:
            if key[0] in 'BbTGP' and key in self.arr:
                if self.arr[key] <= self.t:
                    self.event(key)
                else:
                    self.advance(self.arr[key])
            else:
                self.advance()

    def have(self, keys):
        return all(k in self.done or self.arr.get(k, NEVER) <= self.t for k in keys)

    def spend(self, us):
        self.t += us
        self.poll()

    def take(self):
        out, self.out = self.out, []
        return out

    def run(self):
        pieces = [(t, k, d, n) for t in 'DRSF' for k in BOTH for d in DIRS for n in SIDES]
        order, evs1, evs2 = [], [], []
        self.poll()
        for s, (ch, a) in enumerate(STEPS):
            if ch == 'o':
                while not (c := [p for p in pieces if self.have([('B',) + p])]):
                    later = [self.arr[('B',) + p] for p in pieces if ('B',) + p in self.arr]
                    self.advance(min(later, default=NEVER))
                p = min(c, key=lambda z: self.arr[('B',) + z])
                pieces.remove(p)
                order.append(p)
                self.need(('B',) + p)
            elif a == 0:
                for n in SIDES:
                    for key in [('G', 0, n)] + [('T', q, n) for q in BOTH]:
                        self.need(key)
            evs1.append(self.take())
            if s:
                self.spend(STEP_US)
        loads = [(i, g) for i in range(len(CHUNKS)) for g in range(GROUP)]
        finals = list(range(len(CHUNKS)))

        def load(limit, force=None):
            while loads and loads[0][0] <= limit:
                i, g = loads[0]
                keys = [('b', i, n, ROWS[g]) for n in SIDES]
                if loads[0] != force and not self.have(keys):
                    break
                for key in keys:
                    self.need(key)
                self.out.append(('load', loads.pop(0)))

        def final(limit, force):
            while finals and finals[0] <= limit and (finals[0] <= force or self.have([('P', finals[0], n) for n in SIDES])):
                for n in SIDES:
                    self.need(('P', finals[0], n))
                self.out.append(('final', finals.pop(0)))
                self.t += FINAL_US

        load(1)
        evs1.append(self.take())
        self.spend(STEP_US)
        for i, (_, w) in enumerate(CHUNKS):
            for mine in BOTH:
                for g in range(GROUP):
                    load(i + 1)
                    if not mine and (i, g) in loads:
                        load(i + 1, (i, g))
                    if mine and not g:
                        for n in SIDES:
                            self.push(('x', n), self.sum * w, ('P', i, n))
                        self.poll()
                    if not mine and not g and i > 1:
                        self.out += [('reuse', ('P', i - 2, n)) for n in SIDES]
                    final(i - 1, i - 2 if mine else -1)
                    evs2.append(self.take())
                    self.spend(UNIT_US)
        final(len(CHUNKS), len(CHUNKS))
        return evs1, evs2, self.take(), order


def kernel(side, hid, idx, gate, wg, wu, wd, out, GU, WST, WDB, WDT,
           X, H, own, wbuf, WD, PS, RSB, G, GT, GPT, iv, gv,
           s_in, s_own, s_send, s_link, s_chip, s_way, s_tok, s_gate, s_down, s_dway, s_dchip, s_sum, s_w, s_wd, s_out):
    me = lax.axis_index('ep')
    core, x, y = lax.rem(me, 2), lax.rem(me // 2, side), me // (2 * side)
    tokens, d_model = hid.shape
    half, quarter = tokens // 2, tokens // 4
    ff = wd.shape[1]
    kh, fh = d_model // 2, ff // 2
    item = 2
    planner = Planner(kh * BLOCK * item, fh * item, quarter * d_model * item, HELD * half * 4, half * 4)
    evs1, evs2, tail, order = planner.run()
    rank = {p: i for i, p in enumerate(order)}

    def dev(dx, dy, dc=0):
        row, col = lax.rem(y + dy + side, side), lax.rem(x + dx + side, side)
        return {'ep': (row * side + col) * 2 + lax.rem(core + dc, 2)}

    def part(size, i):
        return pl.ds(i * size, size)

    def column(k, d):
        return (0 if d == 1 else 2) + k

    def expert(n, dy, cc=0):
        return ROWS.index(dy) * GROUP + (1 + n) + cc

    def chunk(i):
        c0, w = CHUNKS[i]
        return c0 // BLOCK, pl.ds(c0 % BLOCK, w)

    def down(i, e):
        b, c = chunk(i)
        return WDB.at[b, e, :, c]

    def down_half(i, n, dy, h):
        b, c = chunk(i)
        return WDB.at[b, expert(n, dy), part(fh, h), c]

    def piece(t, k, d, n, h):
        return GU.at[rank[t, k, d, n], 0, part(kh, h)]

    def copy_of(key, sem=None):
        t, i, *rest = key
        if t == 'G':
            n, = rest
            z = (1 - n) // 2
            return GT.at[part(HELD, 1), part(half, z)], GPT.at[:, part(half, z)], s_gate.at[z], (n, 0)
        if t == 'T':
            n, = rest
            z = (1 - n) + i
            return hid.at[part(quarter, z)], X.at[1, part(quarter, z)], s_tok.at[z], (n, 0)
        if t == 'W':
            d, h = rest
            j = column(i, d)
            return own.at[j, part(kh, h)], WST.at[j, part(kh, h)], s_way.at[j, h], (0, d)
        if t in ('D', 'R', 'S', 'F'):
            d, n, h = rest
            j = column(i, d)
            src, to = {'D': (own.at[j, part(kh, h)], (-n, 0)), 'R': (WST.at[j, part(kh, h)], (-n, 0)),
                       'S': (piece('D', i, d, n, h) if t == 'S' else None, (0, -d)),
                       'F': (piece('R', i, d, n, h) if t == 'F' else None, (0, d))}[t]
            return src, piece(t, i, d, n, h), s_link.at[rank[t, i, d, n], h], to
        if t == 'B':
            a = rank[(i, *rest)]
            return GU.at[a, 0], GU.at[a, 1], s_chip.at[a], (0, 0, 1)
        if t == 'w':
            h, = rest
            b, c = chunk(i)
            c0, w = CHUNKS[i]
            return wd.at[0, part(fh, h), pl.ds(c0, w)], WDT.at[b, part(fh, h), c], s_dway.at[i, h], (0, DIRS[h])
        if t in ('d', 'r', 's', 'f'):
            n, *dy, h = rest
            d = DIRS[h]
            b, c = chunk(i)
            c0, w = CHUNKS[i]
            if t == 'd':
                dy, src, to = 0, wd.at[0, part(fh, h), pl.ds(c0, w)], (-n, 0)
            elif t == 'r':
                dy, src, to = -d, WDT.at[b, part(fh, h), c], (-n, 0)
            elif t == 's':
                dy, = dy
                src, to = down_half(i, n, 0, h), (0, -dy)
            else:
                dy, src, to = 2, down_half(i, n, -d, h), (0, d)
            return src, down_half(i, n, dy, h), s_down.at[i, expert(n, dy) // 2, h], to
        if t == 'b':
            n, dy = rest
            return down(i, expert(n, dy)), down(i, expert(n, dy, 1)), s_dchip.at[i, expert(n, dy) // 2], (0, 0, 1)
        n, = rest
        z = (1 + n) // 2
        b, c = chunk(i)
        _, w = CHUNKS[i]
        return PS.at[1, i % 2, part(half, z), pl.ds(0, w)], RSB.at[b, part(half, z), c], s_sum.at[i, z], (n, 0)

    sent, settled = {}, set()

    def remote(key):
        src, dst, sem, to = copy_of(key)
        return pltpu.make_async_remote_copy(src, dst, s_send.at[sent[key]], sem, device_id=dev(*to), device_id_type=MESH)

    def stage(j, p):
        return pltpu.make_async_copy((wg, wu)[p].at[0, :, part(LANES, j)], own.at[j, :, part(LANES, p)], s_own.at[j, p])

    def bring(i):
        src, dst = ((hid, X.at[0]), (idx, iv), (gate, gv))[i]
        return pltpu.make_async_copy(src, dst, s_in.at[i])

    def tall(rows):
        return jnp.concatenate([rows, jnp.zeros((LANES - HELD, tokens), F32)], axis=0).T

    def build_gates():
        bring(1).wait()
        bring(2).wait()
        shape = (2 * HELD, tokens)
        r, t = lax.broadcasted_iota(jnp.int32, shape, 0), lax.broadcasted_iota(jnp.int32, shape, 1)
        e = lax.rem(r, HELD)
        q = e // GROUP
        dy = jnp.where(q == 1, 1, jnp.where(q == 2, -1, jnp.where(q == 3, 2, 0)))
        shift = jnp.where(r < HELD, 0, jnp.where(t < half, 1, -1)) + 2 * lax.rem(e // 2, 2) - 1
        row, col = lax.rem(y + dy + side, side), lax.rem(x + shift + side, side)
        ids = (row * side + col) * 2 + lax.rem(core + e, 2)
        acc = jnp.zeros(shape, F32)
        for c in range(idx.shape[0]):
            acc = acc + jnp.where(iv[c:c + 1, :] == ids, gv[c:c + 1, :], 0)
        GT[...] = acc
        G[0] = tall(acc[:HELD])

    flags = set()

    def first_time(name):
        new = name not in flags
        flags.add(name)
        return new

    def load_down(par, g, b, c, w):
        return pltpu.make_async_copy(WDB.at[b, part(GROUP, g), :, c], WD.at[par, part(GROUP, g), :, pl.ds(0, w)], s_wd.at[par, g])

    def store(i):
        c = pl.ds(*CHUNKS[i])
        return pltpu.make_async_copy(X.at[0, :, c], out.at[:, c], s_out.at[i])

    def emit(events):
        for kind, key in events:
            if kind == 'send':
                t, k, d, *_ = key
                if t in ('D', 'W') and first_time(column(k, d)):
                    for p in BOTH:
                        stage(column(k, d), p).wait()
                if t == 'G' and first_time('gates'):
                    build_gates()
                sent[key] = len(sent)
                remote(key).start()
            elif kind == 'wait':
                _, dst, sem, _ = copy_of(key)
                pltpu.make_async_copy(dst, dst, sem).wait()
                if key[0] == 'G' and not first_time('partner'):
                    G[1] = tall(GPT[...])
            elif kind == 'load':
                i, g = key
                b, c = chunk(i)
                load_down(i % 2, g, b, c, CHUNKS[i][1]).start()
            elif kind == 'reuse':
                remote(key).wait_send()
                settled.add(key)
            else:
                c0, w = CHUNKS[key]
                b, c = chunk(key)
                for r in range(0, tokens, BLOCK):
                    rows = pl.ds(r, BLOCK)
                    X[0, rows, pl.ds(c0, w)] = (PS[0, key % 2, rows, pl.ds(0, w)] + RSB[b, rows, c]).astype(BF16)
                store(key).start()

    barrier = pltpu.get_barrier_semaphore()
    near = [(1, 0), (-1, 0), (0, 1), (0, -1), (0, 0, 1)]
    for to in near:
        pl.semaphore_signal(barrier, inc=1, device_id=dev(*to), device_id_type=MESH)
    for k in BOTH:
        for d in DIRS:
            for p in BOTH:
                stage(column(k, d), p).start()
    for i in (1, 2, 0):
        bring(i).start()
    pl.semaphore_wait(barrier, len(near))

    def ffn_in(b, a, slot):
        for cc in BOTH:
            for r in range(0, tokens, BLOCK):
                rows = pl.ds(r, BLOCK)
                ab = jnp.dot(X[b, rows, :], wbuf[slot, cc], preferred_element_type=F32)
                u = ab[:, :LANES]
                H[b, a, cc, rows, :] = (u * jax.nn.sigmoid(u) * ab[:, LANES:]).astype(BF16)

    def load_piece(a, slot):
        return pltpu.make_async_copy(GU.at[a], wbuf.at[slot], s_w.at[slot])

    emit(evs1[0])
    bring(0).wait()
    load_piece(0, 0).start()
    first, base = 0, {'o': 0, 'p': 0}
    for si, (pattern, count) in enumerate(SEGMENTS):
        per = {ch: pattern.count(ch) for ch in base}
        after = {ch: base[ch] + per[ch] * count for ch in base}
        follow = SEGMENTS[si + 1][0][0] if si + 1 < len(SEGMENTS) else None

        def body(it, _, first=first, base=base, pattern=pattern, count=count, per=per, after=after, follow=follow):
            for j, ch in enumerate(pattern):
                t = first + it * len(pattern) + j
                a = base[ch] + it * per[ch] + pattern[:j].count(ch)
                for v in range(count):
                    if ev := evs1[first + v * len(pattern) + j + 1]:
                        pl.when(it == v)(lambda ev=ev: emit(ev))
                slot, other = lax.rem(t, 2), lax.rem(t + 1, 2)
                if nxt := pattern[j + 1:j + 2]:
                    load_piece(base[nxt] + it * per[nxt] + pattern[:j + 1].count(nxt), other).start()
                else:
                    nxt = pattern[0]
                    pl.when(it < count - 1)(lambda: load_piece(base[nxt] + (it + 1) * per[nxt], other).start())
                    if follow:
                        pl.when(it == count - 1)(lambda: load_piece(after[follow], other).start())
                load_piece(a, slot).wait()
                ffn_in(0 if ch == 'o' else 1, a, slot)
            return 0

        lax.fori_loop(0, count, body, 0)
        first, base = first + len(pattern) * count, after

    def held(n, dy):
        near_d, far_d = {0: 'DD', 1: 'SR', -1: 'RS', 2: 'FF'}[dy]
        return [rank[near_d, k, 1, n] for k in BOTH] + [rank[far_d, k, -1, n] for k in BOTH]

    def ffn_out(b, par, g, w):
        for q in range(GROUP):
            n, cc = SIDES[q // 2], q % 2
            e = g * GROUP + q
            for r in range(0, tokens, BLOCK):
                rows = pl.ds(r, BLOCK)
                hh = jnp.concatenate([H[b, a, cc, rows, :] for a in held(n, ROWS[g])], axis=1)
                o = jnp.dot(hh, WD[par, e, :, :w], preferred_element_type=F32).astype(BF16).astype(F32)
                ge = G[b, rows, e:e + 1]
                v = jnp.where(ge > 0, ge * o, 0)
                PS[b, par, rows, :w] = v if e == 0 else PS[b, par, rows, :w] + v

    runs = []
    for i, (_, w) in enumerate(CHUNKS):
        if runs and runs[-1][2] == w:
            runs[-1][1] += 1
        else:
            runs.append([i, 1, w])
    for start, count, w in runs:

        def body_down(ib, _, start=start, count=count, w=w):
            b = 1 - lax.rem(ib, 2)
            par = lax.rem(start + ib // 2, 2)
            for g in range(GROUP):
                for v in range(2 * count):
                    if ev := evs2[(2 * start + v) * GROUP + g]:
                        pl.when(ib == v)(lambda ev=ev: emit(ev))
                pl.when(b == 1)(lambda: load_down(par, g, 0, pl.ds(0, w), w).wait())
                ffn_out(b, par, g, w)
            return 0

        lax.fori_loop(0, 2 * count, body_down, 0)
    emit(tail)
    for key in sent:
        if key not in settled:
            remote(key).wait_send()
    for i in range(len(CHUNKS)):
        store(i).wait()


def solution(mesh):
    side = math.isqrt(mesh.shape['ep'] // 2)

    def device_body(hidden, route_idx, gate_weights, w_gate, w_up, w_down):
        tokens, d_model = hidden.shape
        ff = w_gate.shape[2]
        top_k = route_idx.shape[1]
        blocks, nc = d_model // BLOCK, len(CHUNKS)
        shape = jax.ShapeDtypeStruct
        anywhere = pl.BlockSpec(memory_space=pl.ANY)
        dma = pltpu.SemaphoreType.DMA
        columns = ff // LANES
        pairs = HELD // 2
        return pl.pallas_call(
            lambda *refs: kernel(side, *refs),
            out_shape=[shape((tokens, d_model), BF16), shape((PIECES, 2, d_model, BLOCK), BF16),
                       shape((columns, d_model, BLOCK), BF16), shape((blocks, HELD, ff, BLOCK), BF16),
                       shape((blocks, ff, BLOCK), BF16)],
            in_specs=[anywhere] * 6,
            out_specs=[anywhere] * 5,
            scratch_shapes=[
                pltpu.VMEM((2, tokens, d_model), BF16),
                pltpu.VMEM((2, PIECES, 2, tokens, LANES), BF16),
                pltpu.VMEM((columns, d_model, BLOCK), BF16),
                pltpu.VMEM((2, 2, d_model, BLOCK), BF16),
                pltpu.VMEM((2, HELD, ff, BLOCK), BF16),
                pltpu.VMEM((2, 2, tokens, BLOCK), F32),
                pltpu.VMEM((blocks, tokens, BLOCK), F32),
                pltpu.VMEM((2, tokens, LANES), F32),
                pltpu.VMEM((2 * HELD, tokens), F32),
                pltpu.VMEM((HELD, tokens), F32),
                pltpu.VMEM((top_k, tokens), jnp.int32),
                pltpu.VMEM((top_k, tokens), F32),
                dma((3,)), dma((columns, 2)), dma((256,)), dma((PIECES, 2)), dma((PIECES,)), dma((columns, 2)), dma((4,)),
                dma((2,)), dma((nc, pairs, 2)), dma((nc, 2)), dma((nc, pairs)), dma((nc, 2)), dma((2,)), dma((2, GROUP)),
                dma((nc,)),
            ],
            compiler_params=pltpu.CompilerParams(collective_id=0, has_side_effects=True, vmem_limit_bytes=67043328),
            name='moe',
        )(hidden, route_idx.T, gate_weights.T, w_gate, w_up, w_down)[0]

    row_spec = P(('dp', 'ep'), None)
    expert_spec = P('ep', None, None)
    return jax.shard_map(device_body, mesh=mesh, in_specs=(row_spec,) * 3 + (expert_spec,) * 3, out_specs=row_spec, check_vma=False)
```

time: 2440 us -> 230 us (0.09)
  the two profiles are of different devices: /device:TPU:107 before, /device:TPU:97 now
where the time goes in v1:
time: 230 us
  Pallas kernels  227 us (99%)
  local copies, waits for them, and re-layouts  3.08 us (1%)
    pallas_call x1, Pallas kernels, device_body(): pl.pallas_call(lambda *refs: kernel(side, *refs), out_shape=[shape((token...  227 us

profile of v1, /device:TPU:97, one launch (start us, length us, event | category | flops | bytes accessed | tf_op | source)
XLA Modules:
  0.0 230.0 jit_solution(7653737536288619817)
XLA Ops:
  0.0 226.9 %moe.1 = (bf16[1024,1024]{1,0:T(8,128)(2,1)}, bf16[32,2,1024,256]{3,2,1,0:T(8,128)(2,1)}, bf16[4,1024,256]{2,1,0:T(8,128)(2,1)}, bf16[4,16,512,256]{3,2,1,0:T(8,128)(2,1)}, bf16[4,512,256]{2,1,0:T(8,128)(2,1)}) custom-call(bf16[1024,1024]{1,0:T(8,128)(2,1)} %refs_0_.1, s32[8,1024]{1,0:T(8,128)} %bitcast.2, f32[8,1024]{1,0:T(8,128)} %bitcast.3, ...), custom_call_target="tpu_custom_call" | custom-call | tf_op jit(solution)/shard_map/moe/pallas_call | solution.py:505
  226.9 3.1 %copy.8 = bf16[1024,1024]{1,0:T(8,128)(2,1)} copy(bf16[1024,1024]{1,0:T(8,128)(2,1)} %get-tuple-element.6) | data formatting | bytes 4194304

commit v2 on v1

--- a/solution.py
+++ b/solution.py
@@ -19,28 +19,22 @@
 HELD = 16
 PIECES = 32
 ROWS = (0, 1, -1, 2)
-CHUNKS = ((0, 256), (256, 256), (512, 256), (768, 128), (896, 128))
-DETOUR = ()
-LEAD = 12
-SEGMENTS = (('o', LEAD), ('opp', LEAD - 2), ('op', 34 - 2 * LEAD), ('p', 2))
-ORDER = ('W0', 'W1', 'G0', 'D0', 'T0', 'D1', 'd0', 'T1', 'R0', 'R1', 'd1', 'd2', 'd3', 'd4', 'P0', 'P1', 'P2', 'P3', 'P4',
-         'F0', 'S0', 'F1', 'S1', 'f0', 's0', 'f1', 's1', 'f2', 's2', 'f3', 's3', 'f4', 's4')
+CHUNKS = ((0, 256), (256, 256), (512, 256), (768, 256))
+DETOUR = (1,)
+LEAD = 10
+SEGMENTS = (('oo', LEAD // 2), ('opp', LEAD - 2), ('op', PIECES + 2 - 2 * LEAD), ('pp', 1))
+SEGMENTS = tuple(z for z in SEGMENTS if z[1] > 0)
+PARTS = ((0, 3), (3, 4))
+ORDER = ('d0', 'G0', 'T1', 'D1', 'D0', 'T0', 'R0', 'R1', 'd1', 'd2', 'P0', 'P1', 'P2', 'P3', 'r1', 'd3', 's2', 's1',
+         'W1', 'f3', 's0', 'f1', 'w1', 'S1', 'F1', 'f2', 'W0', 'S0', 'F0', 'f0', 's3')
 RANK = {name: i for i, name in enumerate(ORDER)}
-RATE, LATENCY, CHIP_RATE, CHIP_LATENCY = 45.6e3, 2.3, 400e3, 1.8
-STEP_US, UNIT_US, FINAL_US, START_US, AHEAD_US = 1.28, 1.65, 0.6, 5.0, 4.0
+RATE, LATENCY, CHIP_RATE, CHIP_LATENCY, EVENT_US = 46.3e3, 2.8, 400e3, 1.8, 0.015
+PAIR_US, EXPERT_US, DRAIN_US, FINAL_US, START_US, AHEAD_US = 1.09, 0.3, 0.2, 0.6, 5.0, 6.0
+VMEM_BYTES = 64900000
 NEVER, TICK_US = 1e9, 0.01
 
 
-def make_steps():
-    steps, base = [], {'o': 0, 'p': 0}
-    for pattern, count in SEGMENTS:
-        for ch in pattern * count:
-            steps.append((ch, base[ch]))
-            base[ch] += 1
-    return steps
-
-
-STEPS = make_steps()
+STEPS = [pattern for pattern, count in SEGMENTS for _ in range(count)]
 
 
 class Planner:
@@ -79,9 +73,10 @@
                 self.free[link] = max(self.t, self.free.get(link, START_US)) + size / (CHIP_RATE if chip else RATE)
                 self.arr[key] = self.free[link] + (CHIP_LATENCY if chip else LATENCY)
                 self.out.append(('send', key))
+                self.t += EVENT_US
 
     def event(self, key):
-        self.t = max(self.t, self.arr[key])
+        self.t = max(self.t, self.arr[key]) + EVENT_US
         self.out.append(('wait', key))
         self.done.add(key)
         t, i, *rest = key
@@ -160,22 +155,25 @@
         pieces = [(t, k, d, n) for t in 'DRSF' for k in BOTH for d in DIRS for n in SIDES]
         order, evs1, evs2 = [], [], []
         self.poll()
-        for s, (ch, a) in enumerate(STEPS):
-            if ch == 'o':
-                while not (c := [p for p in pieces if self.have([('B',) + p])]):
-                    later = [self.arr[('B',) + p] for p in pieces if ('B',) + p in self.arr]
-                    self.advance(min(later, default=NEVER))
-                p = min(c, key=lambda z: self.arr[('B',) + z])
-                pieces.remove(p)
-                order.append(p)
-                self.need(('B',) + p)
-            elif a == 0:
-                for n in SIDES:
-                    for key in [('G', 0, n)] + [('T', q, n) for q in BOTH]:
-                        self.need(key)
+        partner = False
+        for s, pattern in enumerate(STEPS):
+            for ch in pattern:
+                if ch == 'o':
+                    while not (c := [p for p in pieces if self.have([('B',) + p])]):
+                        later = [self.arr[('B',) + p] for p in pieces if ('B',) + p in self.arr]
+                        self.advance(min(later, default=NEVER))
+                    p = min(c, key=lambda z: self.arr[('B',) + z])
+                    pieces.remove(p)
+                    order.append(p)
+                    self.need(('B',) + p)
+                elif not partner:
+                    partner = True
+                    for n in SIDES:
+                        for key in [('G', 0, n)] + [('T', q, n) for q in BOTH]:
+                            self.need(key)
             evs1.append(self.take())
             if s:
-                self.spend(STEP_US)
+                self.spend(DRAIN_US + PAIR_US * len(STEPS[s - 1]))
         loads = [(i, g) for i in range(len(CHUNKS)) for g in range(GROUP)]
         finals = list(range(len(CHUNKS)))
 
@@ -183,7 +181,7 @@
             while loads and loads[0][0] <= limit:
                 i, g = loads[0]
                 keys = [('b', i, n, ROWS[g]) for n in SIDES]
-                if loads[0] != force and not self.have(keys):
+                if (force is None or loads[0] > force) and not self.have(keys):
                     break
                 for key in keys:
                     self.need(key)
@@ -198,29 +196,32 @@
 
         load(1)
         evs1.append(self.take())
-        self.spend(STEP_US)
+        self.spend(DRAIN_US + PAIR_US * len(STEPS[-1]))
         for i, (_, w) in enumerate(CHUNKS):
             for mine in BOTH:
-                for g in range(GROUP):
+                for begin, end in PARTS:
                     load(i + 1)
-                    if not mine and (i, g) in loads:
-                        load(i + 1, (i, g))
-                    if mine and not g:
+                    if not mine and (i, end - 1) in loads:
+                        load(i + 1, (i, end - 1))
+                    if mine and not begin:
                         for n in SIDES:
                             self.push(('x', n), self.sum * w, ('P', i, n))
                         self.poll()
-                    if not mine and not g and i > 1:
-                        self.out += [('reuse', ('P', i - 2, n)) for n in SIDES]
+                    if not mine and not begin and i > 1:
+                        for n in SIDES:
+                            while ('P', i - 2, n) not in self.arr:
+                                self.advance()
+                            self.out.append(('reuse', ('P', i - 2, n)))
                     final(i - 1, i - 2 if mine else -1)
                     evs2.append(self.take())
-                    self.spend(UNIT_US)
+                    self.spend(DRAIN_US + EXPERT_US * GROUP * (end - begin))
         final(len(CHUNKS), len(CHUNKS))
         return evs1, evs2, self.take(), order
 
 
 def kernel(side, hid, idx, gate, wg, wu, wd, out, GU, WST, WDB, WDT,
            X, H, own, wbuf, WD, PS, RSB, G, GT, GPT, iv, gv,
-           s_in, s_own, s_send, s_link, s_chip, s_way, s_tok, s_gate, s_down, s_dway, s_dchip, s_sum, s_w, s_wd, s_out):
+           s_in, s_own, s_send, s_link, s_chip, s_way, s_tok, s_gate, s_down, s_dway, s_dchip, s_sum, s_w, s_wd):
     me = lax.axis_index('ep')
     core, x, y = lax.rem(me, 2), lax.rem(me // 2, side), me // (2 * side)
     tokens, d_model = hid.shape
@@ -232,9 +233,14 @@
     evs1, evs2, tail, order = planner.run()
     rank = {p: i for i, p in enumerate(order)}
 
-    def dev(dx, dy, dc=0):
+    def device(dx, dy, dc=0):
         row, col = lax.rem(y + dy + side, side), lax.rem(x + dx + side, side)
-        return {'ep': (row * side + col) * 2 + lax.rem(core + dc, 2)}
+        return (row * side + col) * 2 + lax.rem(core + dc, 2)
+
+    near = {to: device(*to) for to in ((1, 0), (-1, 0), (0, 1), (0, -1), (0, 0, 1))}
+
+    def dev(*to):
+        return {'ep': near[to]}
 
     def part(size, i):
         return pl.ds(i * size, size)
@@ -269,7 +275,7 @@
         if t == 'T':
             n, = rest
             z = (1 - n) + i
-            return hid.at[part(quarter, z)], X.at[1, part(quarter, z)], s_tok.at[z], (n, 0)
+            return hid.at[part(quarter, z)], X.at[part(quarter, z)], s_tok.at[z], (n, 0)
         if t == 'W':
             d, h = rest
             j = column(i, d)
@@ -313,7 +319,8 @@
         _, w = CHUNKS[i]
         return PS.at[1, i % 2, part(half, z), pl.ds(0, w)], RSB.at[b, part(half, z), c], s_sum.at[i, z], (n, 0)
 
-    sent, settled = {}, set()
+    sends = [key for events in evs1 + evs2 + [tail] for kind, key in events if kind == 'send']
+    sent, settled = {key: i for i, key in enumerate(sends)}, set()
 
     def remote(key):
         src, dst, sem, to = copy_of(key)
@@ -323,7 +330,7 @@
         return pltpu.make_async_copy((wg, wu)[p].at[0, :, part(LANES, j)], own.at[j, :, part(LANES, p)], s_own.at[j, p])
 
     def bring(i):
-        src, dst = ((hid, X.at[0]), (idx, iv), (gate, gv))[i]
+        src, dst = ((hid, out), (idx, iv), (gate, gv))[i]
         return pltpu.make_async_copy(src, dst, s_in.at[i])
 
     def tall(rows):
@@ -356,10 +363,6 @@
     def load_down(par, g, b, c, w):
         return pltpu.make_async_copy(WDB.at[b, part(GROUP, g), :, c], WD.at[par, part(GROUP, g), :, pl.ds(0, w)], s_wd.at[par, g])
 
-    def store(i):
-        c = pl.ds(*CHUNKS[i])
-        return pltpu.make_async_copy(X.at[0, :, c], out.at[:, c], s_out.at[i])
-
     def emit(events):
         for kind, key in events:
             if kind == 'send':
@@ -369,7 +372,6 @@
                         stage(column(k, d), p).wait()
                 if t == 'G' and first_time('gates'):
                     build_gates()
-                sent[key] = len(sent)
                 remote(key).start()
             elif kind == 'wait':
                 _, dst, sem, _ = copy_of(key)
@@ -388,11 +390,9 @@
                 b, c = chunk(key)
                 for r in range(0, tokens, BLOCK):
                     rows = pl.ds(r, BLOCK)
-                    X[0, rows, pl.ds(c0, w)] = (PS[0, key % 2, rows, pl.ds(0, w)] + RSB[b, rows, c]).astype(BF16)
-                store(key).start()
+                    out[rows, pl.ds(c0, w)] = (PS[0, key % 2, rows, pl.ds(0, w)] + RSB[b, rows, c]).astype(BF16)
 
     barrier = pltpu.get_barrier_semaphore()
-    near = [(1, 0), (-1, 0), (0, 1), (0, -1), (0, 0, 1)]
     for to in near:
         pl.semaphore_signal(barrier, inc=1, device_id=dev(*to), device_id_type=MESH)
     for k in BOTH:
@@ -403,47 +403,50 @@
         bring(i).start()
     pl.semaphore_wait(barrier, len(near))
 
-    def ffn_in(b, a, slot):
+    def ffn_in(b, a, slot, j):
+        rows_in = (out, X)[b]
         for cc in BOTH:
             for r in range(0, tokens, BLOCK):
                 rows = pl.ds(r, BLOCK)
-                ab = jnp.dot(X[b, rows, :], wbuf[slot, cc], preferred_element_type=F32)
+                ab = jnp.dot(rows_in[rows, :], wbuf[slot, j, cc], preferred_element_type=F32)
                 u = ab[:, :LANES]
                 H[b, a, cc, rows, :] = (u * jax.nn.sigmoid(u) * ab[:, LANES:]).astype(BF16)
 
-    def load_piece(a, slot):
-        return pltpu.make_async_copy(GU.at[a], wbuf.at[slot], s_w.at[slot])
+    def load_piece(a, slot, j):
+        return pltpu.make_async_copy(GU.at[a], wbuf.at[slot, j], s_w.at[slot, j])
+
+    def indices(pattern, it, base):
+        return [base[ch] + it * pattern.count(ch) + pattern[:j].count(ch) for j, ch in enumerate(pattern)]
+
+    def load_pieces(pattern, it, base, slot):
+        for j, a in enumerate(indices(pattern, it, base)):
+            load_piece(a, slot, j).start()
 
     emit(evs1[0])
     bring(0).wait()
-    load_piece(0, 0).start()
     first, base = 0, {'o': 0, 'p': 0}
+    load_pieces(STEPS[0], 0, base, 0)
     for si, (pattern, count) in enumerate(SEGMENTS):
-        per = {ch: pattern.count(ch) for ch in base}
-        after = {ch: base[ch] + per[ch] * count for ch in base}
-        follow = SEGMENTS[si + 1][0][0] if si + 1 < len(SEGMENTS) else None
-
-        def body(it, _, first=first, base=base, pattern=pattern, count=count, per=per, after=after, follow=follow):
-            for j, ch in enumerate(pattern):
-                t = first + it * len(pattern) + j
-                a = base[ch] + it * per[ch] + pattern[:j].count(ch)
-                for v in range(count):
-                    if ev := evs1[first + v * len(pattern) + j + 1]:
-                        pl.when(it == v)(lambda ev=ev: emit(ev))
-                slot, other = lax.rem(t, 2), lax.rem(t + 1, 2)
-                if nxt := pattern[j + 1:j + 2]:
-                    load_piece(base[nxt] + it * per[nxt] + pattern[:j + 1].count(nxt), other).start()
-                else:
-                    nxt = pattern[0]
-                    pl.when(it < count - 1)(lambda: load_piece(base[nxt] + (it + 1) * per[nxt], other).start())
-                    if follow:
-                        pl.when(it == count - 1)(lambda: load_piece(after[follow], other).start())
-                load_piece(a, slot).wait()
-                ffn_in(0 if ch == 'o' else 1, a, slot)
+        after = {ch: base[ch] + pattern.count(ch) * count for ch in base}
+        follow = SEGMENTS[si + 1][0] if si + 1 < len(SEGMENTS) else None
+
+        def body(it, _, first=first, base=base, pattern=pattern, count=count, after=after, follow=follow):
+            slot, other = lax.rem(first + it, 2), lax.rem(first + it + 1, 2)
+            for v in range(count):
+                if ev := evs1[first + v + 1]:
+                    pl.when(it == v)(lambda ev=ev: emit(ev))
+            pl.when(it < count - 1)(lambda: load_pieces(pattern, it + 1, base, other))
+            if follow:
+                pl.when(it == count - 1)(lambda: load_pieces(follow, 0, after, other))
+            mine = indices(pattern, it, base)
+            for j, a in enumerate(mine):
+                load_piece(a, slot, j).wait()
+            for j, (ch, a) in enumerate(zip(pattern, mine)):
+                ffn_in(0 if ch == 'o' else 1, a, slot, j)
             return 0
 
         lax.fori_loop(0, count, body, 0)
-        first, base = first + len(pattern) * count, after
+        first, base = first + count, after
 
     def held(n, dy):
         near_d, far_d = {0: 'DD', 1: 'SR', -1: 'RS', 2: 'FF'}[dy]
@@ -472,12 +475,18 @@
         def body_down(ib, _, start=start, count=count, w=w):
             b = 1 - lax.rem(ib, 2)
             par = lax.rem(start + ib // 2, 2)
-            for g in range(GROUP):
+            for z, (begin, end) in enumerate(PARTS):
                 for v in range(2 * count):
-                    if ev := evs2[(2 * start + v) * GROUP + g]:
+                    if ev := evs2[(2 * start + v) * len(PARTS) + z]:
                         pl.when(ib == v)(lambda ev=ev: emit(ev))
-                pl.when(b == 1)(lambda: load_down(par, g, 0, pl.ds(0, w), w).wait())
-                ffn_out(b, par, g, w)
+
+                @pl.when(b == 1)
+                def _():
+                    for g in range(begin, end):
+                        load_down(par, g, 0, pl.ds(0, w), w).wait()
+
+                for g in range(begin, end):
+                    ffn_out(b, par, g, w)
             return 0
 
         lax.fori_loop(0, 2 * count, body_down, 0)
@@ -485,8 +494,6 @@
     for key in sent:
         if key not in settled:
             remote(key).wait_send()
-    for i in range(len(CHUNKS)):
-        store(i).wait()
 
 
 def solution(mesh):
@@ -504,16 +511,16 @@
         pairs = HELD // 2
         return pl.pallas_call(
             lambda *refs: kernel(side, *refs),
-            out_shape=[shape((tokens, d_model), BF16), shape((PIECES, 2, d_model, BLOCK), BF16),
+            out_shape=[pltpu.VMEM((tokens, d_model), BF16), shape((PIECES, 2, d_model, BLOCK), BF16),
                        shape((columns, d_model, BLOCK), BF16), shape((blocks, HELD, ff, BLOCK), BF16),
                        shape((blocks, ff, BLOCK), BF16)],
             in_specs=[anywhere] * 6,
-            out_specs=[anywhere] * 5,
+            out_specs=[pl.BlockSpec(memory_space=pltpu.VMEM)] + [anywhere] * 4,
             scratch_shapes=[
-                pltpu.VMEM((2, tokens, d_model), BF16),
+                pltpu.VMEM((tokens, d_model), BF16),
                 pltpu.VMEM((2, PIECES, 2, tokens, LANES), BF16),
                 pltpu.VMEM((columns, d_model, BLOCK), BF16),
-                pltpu.VMEM((2, 2, d_model, BLOCK), BF16),
+                pltpu.VMEM((2, 3, 2, d_model, BLOCK), BF16),
                 pltpu.VMEM((2, HELD, ff, BLOCK), BF16),
                 pltpu.VMEM((2, 2, tokens, BLOCK), F32),
                 pltpu.VMEM((blocks, tokens, BLOCK), F32),
@@ -523,10 +530,9 @@
                 pltpu.VMEM((top_k, tokens), jnp.int32),
                 pltpu.VMEM((top_k, tokens), F32),
                 dma((3,)), dma((columns, 2)), dma((256,)), dma((PIECES, 2)), dma((PIECES,)), dma((columns, 2)), dma((4,)),
-                dma((2,)), dma((nc, pairs, 2)), dma((nc, 2)), dma((nc, pairs)), dma((nc, 2)), dma((2,)), dma((2, GROUP)),
-                dma((nc,)),
+                dma((2,)), dma((nc, pairs, 2)), dma((nc, 2)), dma((nc, pairs)), dma((nc, 2)), dma((2, 3)), dma((2, GROUP)),
             ],
-            compiler_params=pltpu.CompilerParams(collective_id=0, has_side_effects=True, vmem_limit_bytes=67043328),
+            compiler_params=pltpu.CompilerParams(collective_id=0, has_side_effects=True, vmem_limit_bytes=VMEM_BYTES),
             name='moe',
         )(hidden, route_idx.T, gate_weights.T, w_gate, w_up, w_down)[0]
 

time: 230 us -> 214 us (0.930)
  Pallas kernels: 227 us -> 213 us
    pallas_call x1, Pallas kernels: 227 us -> 213 us  [device_body(): pl.pallas_call(lambda *refs: kernel(side, *refs), out_shape=[pltpu.VMEM((...]
where the time goes in v2:
time: 214 us
  Pallas kernels  213 us (100%)
    pallas_call x1, Pallas kernels, device_body(): pl.pallas_call(lambda *refs: kernel(side, *refs), out_shape=[pltpu.VMEM((...  213 us

profile of v2, /device:TPU:97, one launch (start us, length us, event | category | flops | bytes accessed | tf_op | source)
XLA Modules:
  0.0 214.3 jit_solution(10682905473771461088)
XLA Ops:
  0.0 212.9 %moe.1 = (bf16[1024,1024]{1,0:T(8,128)(2,1)S(1)}, bf16[32,2,1024,256]{3,2,1,0:T(8,128)(2,1)}, bf16[4,1024,256]{2,1,0:T(8,128)(2,1)}, bf16[4,16,512,256]{3,2,1,0:T(8,128)(2,1)}, bf16[4,512,256]{2,1,0:T(8,128)(2,1)}) custom-call(bf16[1024,1024]{1,0:T(8,128)(2,1)} %refs_0_.1, s32[8,1024]{1,0:T(8,128)} %bitcast.2, f32[8,1024]{1,0:T(8,128)} %bitcast.3, ...), custom_call_target="tpu_custom_call" | custom-call | tf_op jit(solution)/shard_map/moe/pallas_call | solution.py:512
  212.9 1.3 copy.8

commit v3 on v2

--- a/solution.py
+++ b/solution.py
@@ -19,19 +19,25 @@
 HELD = 16
 PIECES = 32
 ROWS = (0, 1, -1, 2)
-CHUNKS = ((0, 256), (256, 256), (512, 256), (768, 256))
-DETOUR = (1,)
-LEAD = 10
+CHUNKS = ((0, 256), (256, 256), (512, 256), (768, 128), (896, 128))
+TURNS = ((1, (0,)), (0, (0,)), (1, (1,)), (0, (1,)), (1, (2,)), (0, (2,)), (1, (3,)), (1, (4,)), (0, (3, 4)))
+DETOUR = (0, 1, 2)
+LEAD = 12
 SEGMENTS = (('oo', LEAD // 2), ('opp', LEAD - 2), ('op', PIECES + 2 - 2 * LEAD), ('pp', 1))
 SEGMENTS = tuple(z for z in SEGMENTS if z[1] > 0)
 PARTS = ((0, 3), (3, 4))
-ORDER = ('d0', 'G0', 'T1', 'D1', 'D0', 'T0', 'R0', 'R1', 'd1', 'd2', 'P0', 'P1', 'P2', 'P3', 'r1', 'd3', 's2', 's1',
-         'W1', 'f3', 's0', 'f1', 'w1', 'S1', 'F1', 'f2', 'W0', 'S0', 'F0', 'f0', 's3')
+ORDER = ('D0', 'G0', 'D1', 'T0', 'T1', 'R1', 'R0', 'd0', 'r0', 'd1', 'P0', 'P1', 'P2', 'P3', 'P4', 'r1', 'd2', 'r2',
+         'd3', 'd4', 'W1', 'W0', 'F1', 'f3', 'w1', 's3', 'f0', 'f4', 'S1', 'w0', 'f1', 's4', 'S0', 's2', 'w2', 'F0',
+         's1', 's0', 'f2')
 RANK = {name: i for i, name in enumerate(ORDER)}
 RATE, LATENCY, CHIP_RATE, CHIP_LATENCY, EVENT_US = 46.3e3, 2.8, 400e3, 1.8, 0.015
-PAIR_US, EXPERT_US, DRAIN_US, FINAL_US, START_US, AHEAD_US = 1.09, 0.3, 0.2, 0.6, 5.0, 6.0
+PAIR_US, EXPERT_US, DRAIN_US, FINAL_US, START_US, AHEAD_US = 1.13, 0.315, 0.22, 0.6, 5.0, 12.0
 VMEM_BYTES = 64900000
-NEVER, TICK_US = 1e9, 0.01
+NEVER, TICK_US, EARLY_US, SETTLED_US = 1e9, 0.01, 0.0, 3.0
+
+
+def block(i):
+    return CHUNKS[i][0] // BLOCK
 
 
 STEPS = [pattern for pattern, count in SEGMENTS for _ in range(count)]
@@ -40,7 +46,7 @@
 class Planner:
     def __init__(self, piece_bytes, down_bytes, token_bytes, gate_bytes, sum_bytes):
         self.t, self.free, self.arr, self.ready, self.done, self.out = START_US, {}, {}, {}, set(), []
-        self.piece, self.sum = piece_bytes, sum_bytes
+        self.piece, self.sum, self.unsettled = piece_bytes, sum_bytes, []
         self.down = [down_bytes * w for _, w in CHUNKS]
         for n in SIDES:
             self.push(('x', n), gate_bytes, ('G', 0, n))
@@ -74,6 +80,8 @@
                 self.arr[key] = self.free[link] + (CHIP_LATENCY if chip else LATENCY)
                 self.out.append(('send', key))
                 self.t += EVENT_US
+                if key[0] != 'P':
+                    self.unsettled.append(key)
 
     def event(self, key):
         self.t = max(self.t, self.arr[key]) + EVENT_US
@@ -125,6 +133,9 @@
         self.fill()
 
     def advance(self, upto=NEVER):
+        while self.unsettled and self.arr[self.unsettled[0]] <= self.t - SETTLED_US:
+            self.out.append(('settle', self.unsettled.pop(0)))
+            self.t += EVENT_US
         p = self.next_event()
         c = [self.free.get(link, START_US) - AHEAD_US + TICK_US for link, queue in self.ready.items() if queue]
         self.t = max(self.t, min([p[0] if p else NEVER, upto] + c))
@@ -140,8 +151,8 @@
             else:
                 self.advance()
 
-    def have(self, keys):
-        return all(k in self.done or self.arr.get(k, NEVER) <= self.t for k in keys)
+    def have(self, keys, early=0.0):
+        return all(k in self.done or self.arr.get(k, NEVER) <= self.t + early for k in keys)
 
     def spend(self, us):
         self.t += us
@@ -155,7 +166,7 @@
         pieces = [(t, k, d, n) for t in 'DRSF' for k in BOTH for d in DIRS for n in SIDES]
         order, evs1, evs2 = [], [], []
         self.poll()
-        partner = False
+        partner, reused = False, set()
         for s, pattern in enumerate(STEPS):
             for ch in pattern:
                 if ch == 'o':
@@ -175,47 +186,56 @@
             if s:
                 self.spend(DRAIN_US + PAIR_US * len(STEPS[s - 1]))
         loads = [(i, g) for i in range(len(CHUNKS)) for g in range(GROUP)]
-        finals = list(range(len(CHUNKS)))
-
-        def load(limit, force=None):
-            while loads and loads[0][0] <= limit:
+        finals, summed = list(range(len(CHUNKS))), set()
+
+        def load(force=None):
+            while loads:
                 i, g = loads[0]
                 keys = [('b', i, n, ROWS[g]) for n in SIDES]
-                if (force is None or loads[0] > force) and not self.have(keys):
+                forced = force is not None and loads[0] <= force
+                room = all(c in summed for c in range(i) if block(c) <= block(i) - 2)
+                if not room or not (forced or self.have(keys, EARLY_US)):
                     break
                 for key in keys:
                     self.need(key)
                 self.out.append(('load', loads.pop(0)))
 
-        def final(limit, force):
-            while finals and finals[0] <= limit and (finals[0] <= force or self.have([('P', finals[0], n) for n in SIDES])):
+        def final(force=-1):
+            while finals and finals[0] in summed and (finals[0] <= force or self.have([('P', finals[0], n) for n in SIDES])):
                 for n in SIDES:
                     self.need(('P', finals[0], n))
                 self.out.append(('final', finals.pop(0)))
                 self.t += FINAL_US
 
-        load(1)
+        load()
         evs1.append(self.take())
         self.spend(DRAIN_US + PAIR_US * len(STEPS[-1]))
-        for i, (_, w) in enumerate(CHUNKS):
-            for mine in BOTH:
-                for begin, end in PARTS:
-                    load(i + 1)
-                    if not mine and (i, end - 1) in loads:
-                        load(i + 1, (i, end - 1))
-                    if mine and not begin:
-                        for n in SIDES:
-                            self.push(('x', n), self.sum * w, ('P', i, n))
-                        self.poll()
-                    if not mine and not begin and i > 1:
-                        for n in SIDES:
-                            while ('P', i - 2, n) not in self.arr:
-                                self.advance()
-                            self.out.append(('reuse', ('P', i - 2, n)))
-                    final(i - 1, i - 2 if mine else -1)
-                    evs2.append(self.take())
-                    self.spend(DRAIN_US + EXPERT_US * GROUP * (end - begin))
-        final(len(CHUNKS), len(CHUNKS))
+        for b, chunks in TURNS:
+            for begin, end in PARTS:
+                load()
+                old = [c for c in range(chunks[0]) if block(c) <= block(chunks[0]) - 2]
+                if b:
+                    load((chunks[0], end - 1))
+                    for i in old if not begin else ():
+                        if i not in reused:
+                            reused.add(i)
+                            for n in SIDES:
+                                while ('P', i, n) not in self.arr:
+                                    self.advance()
+                                self.out.append(('reuse', ('P', i, n)))
+                    final()
+                else:
+                    final(max(old, default=-1))
+                evs2.append(self.take())
+                self.spend(DRAIN_US + EXPERT_US * GROUP * (end - begin))
+            for i in chunks:
+                if b:
+                    for n in SIDES:
+                        self.push(('x', n), self.sum * CHUNKS[i][1], ('P', i, n))
+                else:
+                    summed.add(i)
+            self.poll()
+        final(len(CHUNKS))
         return evs1, evs2, self.take(), order
 
 
@@ -316,8 +336,7 @@
         n, = rest
         z = (1 + n) // 2
         b, c = chunk(i)
-        _, w = CHUNKS[i]
-        return PS.at[1, i % 2, part(half, z), pl.ds(0, w)], RSB.at[b, part(half, z), c], s_sum.at[i, z], (n, 0)
+        return PS.at[1, b % 2, part(half, z), c], RSB.at[b, part(half, z), c], s_sum.at[i, z], (n, 0)
 
     sends = [key for events in evs1 + evs2 + [tail] for kind, key in events if kind == 'send']
     sent, settled = {key: i for i, key in enumerate(sends)}, set()
@@ -360,8 +379,8 @@
         flags.add(name)
         return new
 
-    def load_down(par, g, b, c, w):
-        return pltpu.make_async_copy(WDB.at[b, part(GROUP, g), :, c], WD.at[par, part(GROUP, g), :, pl.ds(0, w)], s_wd.at[par, g])
+    def load_down(par, g, b, c, sub):
+        return pltpu.make_async_copy(WDB.at[b, part(GROUP, g), :, c], WD.at[par, part(GROUP, g), :, c], s_wd.at[par, g, sub])
 
     def emit(events):
         for kind, key in events:
@@ -381,8 +400,8 @@
             elif kind == 'load':
                 i, g = key
                 b, c = chunk(i)
-                load_down(i % 2, g, b, c, CHUNKS[i][1]).start()
-            elif kind == 'reuse':
+                load_down(b % 2, g, b, c, CHUNKS[i][0] % BLOCK // LANES).start()
+            elif kind in ('reuse', 'settle'):
                 remote(key).wait_send()
                 settled.add(key)
             else:
@@ -390,7 +409,7 @@
                 b, c = chunk(key)
                 for r in range(0, tokens, BLOCK):
                     rows = pl.ds(r, BLOCK)
-                    out[rows, pl.ds(c0, w)] = (PS[0, key % 2, rows, pl.ds(0, w)] + RSB[b, rows, c]).astype(BF16)
+                    out[rows, pl.ds(c0, w)] = (PS[0, b % 2, rows, c] + RSB[b, rows, c]).astype(BF16)
 
     barrier = pltpu.get_barrier_semaphore()
     for to in near:
@@ -452,45 +471,54 @@
         near_d, far_d = {0: 'DD', 1: 'SR', -1: 'RS', 2: 'FF'}[dy]
         return [rank[near_d, k, 1, n] for k in BOTH] + [rank[far_d, k, -1, n] for k in BOTH]
 
-    def ffn_out(b, par, g, w):
+    def ffn_out(b, par, g, c):
         for q in range(GROUP):
             n, cc = SIDES[q // 2], q % 2
             e = g * GROUP + q
             for r in range(0, tokens, BLOCK):
                 rows = pl.ds(r, BLOCK)
                 hh = jnp.concatenate([H[b, a, cc, rows, :] for a in held(n, ROWS[g])], axis=1)
-                o = jnp.dot(hh, WD[par, e, :, :w], preferred_element_type=F32).astype(BF16).astype(F32)
+                o = jnp.dot(hh, WD[par, e, :, c], preferred_element_type=F32).astype(BF16).astype(F32)
                 ge = G[b, rows, e:e + 1]
                 v = jnp.where(ge > 0, ge * o, 0)
-                PS[b, par, rows, :w] = v if e == 0 else PS[b, par, rows, :w] + v
-
-    runs = []
-    for i, (_, w) in enumerate(CHUNKS):
-        if runs and runs[-1][2] == w:
-            runs[-1][1] += 1
-        else:
-            runs.append([i, 1, w])
-    for start, count, w in runs:
-
-        def body_down(ib, _, start=start, count=count, w=w):
-            b = 1 - lax.rem(ib, 2)
-            par = lax.rem(start + ib // 2, 2)
-            for z, (begin, end) in enumerate(PARTS):
-                for v in range(2 * count):
-                    if ev := evs2[(2 * start + v) * len(PARTS) + z]:
-                        pl.when(ib == v)(lambda ev=ev: emit(ev))
-
-                @pl.when(b == 1)
-                def _():
-                    for g in range(begin, end):
-                        load_down(par, g, 0, pl.ds(0, w), w).wait()
-
+                PS[b, par, rows, c] = v if e == 0 else PS[b, par, rows, c] + v
+
+    def sums(b, par, c, sub, turns, v):
+        for z, (begin, end) in enumerate(PARTS):
+            for u in turns:
+                if ev := evs2[u * len(PARTS) + z]:
+                    pl.when(v == u)(lambda ev=ev: emit(ev))
+
+            @pl.when(b == 1)
+            def _():
                 for g in range(begin, end):
-                    ffn_out(b, par, g, w)
-            return 0
-
-        lax.fori_loop(0, 2 * count, body_down, 0)
-    emit(tail)
+                    load_down(par, g, 0, c, sub).wait()
+
+            for g in range(begin, end):
+                ffn_out(b, par, g, c)
+
+    whole = [u for u, (_, chunks) in enumerate(TURNS) if CHUNKS[chunks[0]][1] == BLOCK]
+    parts = [u for u, (b, _) in enumerate(TURNS) if b and u not in whole]
+    last = len(TURNS) - 1
+    par = block(len(CHUNKS) - 1) % 2
+
+    def body_whole(v, _):
+        sums(1 - lax.rem(v, 2), lax.rem(v // 2, 2), pl.ds(0, BLOCK), 0, whole, v)
+        return 0
+
+    def body_parts(v, _):
+        sub = v - len(whole)
+        sums(1, par, pl.ds(pl.multiple_of(sub * LANES, LANES), LANES), sub, parts, v)
+        return 0
+
+    lax.fori_loop(0, len(whole), body_whole, 0)
+    lax.fori_loop(len(whole), last, body_parts, 0)
+    sums(0, par, pl.ds(0, BLOCK), 0, (last,), last)
+    for key in sent:
+        if key not in settled and key[0] != 'P':
+            remote(key).wait_send()
+            settled.add(key)
+    emit([event for event in tail if event[0] != 'settle'])
     for key in sent:
         if key not in settled:
             remote(key).wait_send()
@@ -530,7 +558,7 @@
                 pltpu.VMEM((top_k, tokens), jnp.int32),
                 pltpu.VMEM((top_k, tokens), F32),
                 dma((3,)), dma((columns, 2)), dma((256,)), dma((PIECES, 2)), dma((PIECES,)), dma((columns, 2)), dma((4,)),
-                dma((2,)), dma((nc, pairs, 2)), dma((nc, 2)), dma((nc, pairs)), dma((nc, 2)), dma((2, 3)), dma((2, GROUP)),
+                dma((2,)), dma((nc, pairs, 2)), dma((nc, 2)), dma((nc, pairs)), dma((nc, 2)), dma((2, 3)), dma((2, GROUP, 2)),
             ],
             compiler_params=pltpu.CompilerParams(collective_id=0, has_side_effects=True, vmem_limit_bytes=VMEM_BYTES),
             name='moe',

time: 214 us -> 212 us (level)
  Pallas kernels: 213 us -> 209 us
    pallas_call x1, Pallas kernels: 213 us -> 209 us  [device_body(): pl.pallas_call(lambda *refs: kernel(side, *refs), out_shape=[pltpu.VMEM((...]
where the time goes in v3:
time: 212 us; the launch traced here: 211 us
  Pallas kernels  209 us (99%)
    pallas_call x1, Pallas kernels, device_body(): pl.pallas_call(lambda *refs: kernel(side, *refs), out_shape=[pltpu.VMEM((...  209 us

profile of v3, /device:TPU:97, one launch (start us, length us, event | category | flops | bytes accessed | tf_op | source)
XLA Modules:
  0.0 210.6 jit_solution(16801658385816041781)
XLA Ops:
  0.0 209.2 %moe.1 = (bf16[1024,1024]{1,0:T(8,128)(2,1)S(1)}, bf16[32,2,1024,256]{3,2,1,0:T(8,128)(2,1)}, bf16[4,1024,256]{2,1,0:T(8,128)(2,1)}, bf16[4,16,512,256]{3,2,1,0:T(8,128)(2,1)}, bf16[4,512,256]{2,1,0:T(8,128)(2,1)}) custom-call(bf16[1024,1024]{1,0:T(8,128)(2,1)} %refs_0_.1, s32[8,1024]{1,0:T(8,128)} %bitcast.2, f32[8,1024]{1,0:T(8,128)} %bitcast.3, ...), custom_call_target="tpu_custom_call" | custom-call | tf_op jit(solution)/shard_map/moe/pallas_call | solution.py:540
  209.2 1.3 copy.8
